TPU v7x, 32 devices: a whole 2x2x4 slice. The times are simulated.
32 devices in a mesh: dp: 16 (over z, x, core), tensor: 2 (over y).
Axes of the slice: x: 2, y: 2, z: 4, core: 2. Of those that a mesh axis runs over, the one named last changes fastest.
Arguments:
- query_rows: bfloat16 [6144, 5120], P('dp', 'tensor'), may hold values from -128 to 128
- key_rows: bfloat16 [6144, 5120], P('dp', 'tensor'), may hold values from -5 to 5
- value_rows: bfloat16 [6144, 5120], P('dp', 'tensor'), may hold values from -12 to 12
- action_mask: int32 [16, 384], P('dp'), may hold values from 0 to 1, as said below
- residual: bfloat16 [6144, 5120], P('dp', 'tensor'), may hold values from -100 to 100
- out_weight: bfloat16 [5120, 5120], P(None, 'tensor'), may hold values from -0.078125 to 0.078125
- norm_gain: float32 [5120], P('tensor'), may hold values from 0.1 to 1.9
- upstream: bfloat16 [6144, 5120], P('dp', 'tensor'), may hold values from -6 to 6
- residual_grad: bfloat16 [6144, 5120], P('dp', 'tensor'), may hold values from -2 to 2
Outputs:
- layer_out: bfloat16 [6144, 5120], P('dp', 'tensor')
- grad_residual: bfloat16 [6144, 5120], P('dp', 'tensor')
- grad_query: bfloat16 [6144, 5120], P('dp', 'tensor')
- grad_key: bfloat16 [6144, 5120], P('dp', 'tensor')
- grad_value: bfloat16 [6144, 5120], P('dp', 'tensor')
- grad_out_weight: float32 [5120, 5120], P('dp', 'tensor')
- grad_gain: float32 [5120], P('tensor')
Inputs may be any that keep to these rules, and one draw needn't show every extreme that they name: `action_mask`: each row is a run of zeros followed by a run of ones; the ones number 1 to 192.
All inputs are finite; a program needn't handle non-finite values.
Results may differ from a plain program's by a relative error of at most 0.015.
Values may be sent and summed in bfloat16 or wider, within the bound.
A program may use at most 192 MiB of HBM per device.

v0:
```python
import jax
import jax.numpy as jnp
from jax import lax
from jax.sharding import PartitionSpec as P

D = 5120
HEAD_DIM = 128
LEN = 384


epsilon = 1e-05


def visible(mask_row):
    position = jnp.arange(mask_row.shape[0])
    causal = position[None, :] <= position[:, None]
    observe = mask_row == 0
    return causal | observe[:, None] & observe[None, :]


def shards(
    query_rows,
    key_rows,
    value_rows,
    action_mask,
    residual,
    out_weight,
    norm_gain,
    upstream,
    residual_grad,
):
    seq_count = action_mask.shape[0]
    tok_rows = query_rows.shape[0]
    local_width = query_rows.shape[1]
    head_shape = (seq_count, LEN, local_width // HEAD_DIM, HEAD_DIM)
    query_heads = query_rows.reshape(head_shape)
    key_heads = key_rows.reshape(head_shape)
    value_heads = value_rows.reshape(head_shape)
    score_scale = HEAD_DIM ** (-0.5)
    allowed = jax.vmap(visible)(action_mask)
    scores = (
        jnp.einsum("sqhd,skhd->shqk", query_heads, key_heads, preferred_element_type=jnp.float32)
        * score_scale
    )
    masked = jnp.where(allowed[:, None], scores, -jnp.inf)
    row_top = jnp.max(masked, axis=-1, keepdims=True)
    weights = jnp.exp(masked - row_top)
    chances = weights / jnp.sum(weights, axis=-1, keepdims=True)
    chances_low = chances.astype(jnp.bfloat16)
    attended = jnp.einsum(
        "shqk,skhd->sqhd", chances_low, value_heads, preferred_element_type=jnp.float32
    )
    attended = attended.astype(jnp.bfloat16).reshape(tok_rows, local_width)
    projected = jnp.dot(attended, out_weight.T, preferred_element_type=jnp.float32)
    own_width = residual.shape[1]
    full_sum = lax.psum(projected, "tensor")
    own_sum = lax.dynamic_slice_in_dim(full_sum, lax.axis_index("tensor") * own_width, own_width, 1)
    layer_out = (own_sum + residual.astype(jnp.float32)).astype(jnp.bfloat16)
    out_float = layer_out.astype(jnp.float32)
    upstream_float = upstream.astype(jnp.float32)
    scaled = upstream_float * norm_gain[None, :]
    square_sum, inner_sum = lax.psum(
        (jnp.sum(out_float * out_float, axis=1), jnp.sum(scaled * out_float, axis=1)), "tensor"
    )
    row_rms = jnp.sqrt(square_sum / D + epsilon)[:, None]
    normed = out_float / row_rms
    row_inner = inner_sum[:, None] / (row_rms * D)
    grad_residual = (
        residual_grad.astype(jnp.float32) + (scaled - normed * row_inner) / row_rms
    ).astype(jnp.bfloat16)
    grad_gain = lax.psum(jnp.sum(upstream_float * normed, axis=0), "dp")
    grad_full = lax.all_gather(grad_residual, "tensor", axis=1, tiled=True)
    grad_attended = jnp.dot(grad_full, out_weight, preferred_element_type=jnp.float32).astype(
        jnp.bfloat16
    )
    contract_rows = (((0,), (0,)), ((), ()))
    received = lax.all_to_all(grad_full, "dp", split_axis=1, concat_axis=0, tiled=True)
    grad_out_weight = lax.dot_general(
        received,
        lax.all_gather(attended, "dp", axis=0, tiled=True),
        contract_rows,
        preferred_element_type=jnp.float32,
    )
    grad_heads = grad_attended.reshape(head_shape)
    grad_value = jnp.einsum(
        "shqk,sqhd->skhd", chances_low, grad_heads, preferred_element_type=jnp.float32
    ).astype(jnp.bfloat16)
    grad_chances = jnp.einsum(
        "sqhd,skhd->shqk", grad_heads, value_heads, preferred_element_type=jnp.float32
    )
    row_delta = jnp.sum(chances * grad_chances, axis=-1, keepdims=True)
    grad_scores = (chances * (grad_chances - row_delta) * score_scale).astype(jnp.bfloat16)
    grad_query = jnp.einsum(
        "shqk,skhd->sqhd", grad_scores, key_heads, preferred_element_type=jnp.float32
    ).astype(jnp.bfloat16)
    grad_key = jnp.einsum(
        "shqk,sqhd->skhd", grad_scores, query_heads, preferred_element_type=jnp.float32
    ).astype(jnp.bfloat16)
    return (
        layer_out,
        grad_residual,
        grad_query.reshape(tok_rows, local_width),
        grad_key.reshape(tok_rows, local_width),
        grad_value.reshape(tok_rows, local_width),
        grad_out_weight,
        grad_gain,
    )


def solution(mesh):
    placed = (
        P("dp", "tensor"),
        P("dp", "tensor"),
        P("dp", "tensor"),
        P("dp", None),
        P("dp", "tensor"),
        P(None, "tensor"),
        P("tensor"),
        P("dp", "tensor"),
        P("dp", "tensor"),
    )
    return jax.shard_map(
        shards,
        mesh=mesh,
        in_specs=placed,
        out_specs=(
            P("dp", "tensor"),
            P("dp", "tensor"),
            P("dp", "tensor"),
            P("dp", "tensor"),
            P("dp", "tensor"),
            P("dp", "tensor"),
            P("tensor"),
        ),
        check_vma=False,
    )
```

profile of v0, /device:TPU:0, one launch (start us, length us, event | category | flops | bytes accessed | tf_op | source)
XLA Modules:
  0.0 635.0 jit_solution(9114788977476758334)
XLA Ops:
  7.2 0.0 copy-start.6
  7.2 0.0 all-reduce.2.cloned.1.call-start
  7.2 2.8 copy.35
  10.1 0.0 copy-done.6
  10.1 0.0 copy-start.1
  10.1 0.1 fusion.40
  10.3 4.4 copy.31
  14.7 3.9 copy.32
  18.6 10.4 %fusion.47 = (f32[20,384]{1,0:T(8,128)S(1)}, f32[20,384,384]{1,2,0:T(8,128)}) fusion(pred[384,384]{0,1:T(8,128)(4,1)S(1)} %fusion.40, bf16[384,20,128]{0,2,1:T(8,128)(2,1)} %bitcast.58, bf16[384,20,128]{0,2,1:T(8,128)(2,1)} %bitcast.60), kind=kOutput, calls=%fused_computation.48 | convolution fusion | flops 766771584 | bytes 15906816 | tf_op jit(solution)/shard_map/sub | solution.py:47
  29.0 0.0 copy-done.1
  29.0 7.1 %fusion.26 = bf16[20,384,128]{1,2,0:T(8,128)(2,1)} fusion(bf16[384,20,128]{0,2,1:T(8,128)(2,1)S(1)} %bitcast.51, f32[20,384,384]{1,2,0:T(8,128)} %get-tuple-element.26, f32[20,384]{1,0:T(8,128)S(1)} %get-tuple-element.25), kind=kOutput, calls=%fused_computation.32 | convolution fusion | flops 761856000 | bytes 15759360 | tf_op jit(solution)/shard_map/shqk,skhd->sqhd/dot_general | solution.py:50
  36.1 17.8 %fusion.48 = f32[384,5120]{1,0:T(8,128)} fusion(bf16[384,2560]{0,1:T(8,128)(2,1)} %bitcast.56, bf16[5120,2560]{1,0:T(8,128)(2,1)} %param.14), kind=kOutput, calls=%fused_computation.49 | convolution fusion | flops 10066329600 | bytes 36044800 | tf_op jit(solution)/shard_map/dot_general | solution.py:54
  53.9 0.0 all-reduce.2.cloned.1.call-update
  54.0 0.2 all-gather.3.cloned.1.call-start
  54.2 0.0 copy-start.5
  54.2 189.9 %all-reduce.2.cloned.1.call-done = f32[384,5120]{1,0:T(8,128)} async-done(((f32[384,5120]{1,0:T(8,128)}), f32[384,5120]{1,0:T(8,128)}) %all-reduce.2.cloned.1.call-update) | async-done | bytes 7864336 | tf_op jit(solution)/shard_map/psum | solution.py:56
  244.1 3.4 fusion.19
  247.5 0.0 copy-start
  247.5 4.9 psum.29
  252.5 0.0 copy-done.5
  252.5 3.1 fusion.18
  255.5 4.9 psum.30
  260.5 5.0 fusion.21
  265.4 0.0 copy-done
  265.4 0.0 all-gather.3.cloned.1.call-update
  265.5 0.0 all-gather.5.cloned.1.call-start
  265.5 0.7 all-gather.5.cloned.1.call-update
  266.2 53.2 %all-gather.3.cloned.1.call-done = bf16[384,5120]{1,0:T(8,128)(2,1)} async-done(((bf16[384,2560]{1,0:T(8,128)(2,1)}), bf16[384,5120]{1,0:T(8,128)(2,1)}) %all-gather.3.cloned.1.call-update) | async-done | bytes 3932176 | tf_op jit(solution)/shard_map/all_gather | solution.py:72
  319.4 6.3 copy.43
  325.7 5.7 all-to-all-start
  331.3 185.8 %psum.31 = f32[2560]{0:T(1024)} all-reduce(f32[2560]{0:T(1024)S(1)} %get-tuple-element.21), channel_id=1, replica_groups=mesh['dp'=16,'tensor'=2] {'dp'}, use_global_device_ids=true, to_apply=%region_9.10 | all-reduce | flops 2560 | bytes 20480 | tf_op jit(solution)/shard_map/psum | solution.py:71
  517.1 17.4 %convolution_convert_fusion = bf16[384,2560]{1,0:T(8,128)(2,1)} fusion(bf16[384,5120]{1,0:T(8,128)(2,1)} %all-gather.3.cloned.1.call-done, bf16[5120,2560]{1,0:T(8,128)(2,1)} %param.14), kind=kOutput, calls=%fused_computation.20 | convolution fusion | flops 10067312640 | bytes 32112640 | tf_op jit(solution)/shard_map/dot_general | solution.py:73
  534.5 0.0 copy-start.2
  534.5 4.2 copy.37
  538.7 0.0 copy-done.2
  538.7 7.6 %fusion.49 = f32[20,384,384]{1,2,0:T(8,128)} fusion(bf16[384,20,128]{0,2,1:T(8,128)(2,1)} %bitcast.53, bf16[384,20,128]{0,2,1:T(8,128)(2,1)S(1)} %bitcast.52), kind=kOutput, calls=%fused_computation.50 | convolution fusion | flops 754974720 | bytes 15728640 | tf_op jit(solution)/shard_map/sqhd,skhd->shqk/dot_general | solution.py:88
  546.3 20.3 %fusion.32 = bf16[20,384,128]{1,2,0:T(8,128)(2,1)} fusion(bf16[384,20,128]{0,2,1:T(8,128)(2,1)} %bitcast.61, f32[20,384,384]{1,2,0:T(8,128)} %fusion.49, f32[20,384,384]{1,2,0:T(8,128)} %get-tuple-element.26, f32[20,384]{1,0:T(8,128)S(1)} %get-tuple-element.25), kind=kOutput, calls=%fused_computation.34 | convolution fusion | flops 776609664 | bytes 27555840 | tf_op jit(solution)/shard_map/shqk,skhd->sqhd/dot_general | solution.py:93
  566.6 0.0 copy-start.4
  566.6 4.1 copy.45
  570.7 0.0 copy-done.4
  570.7 19.7 %fusion.35 = bf16[20,384,128]{1,2,0:T(8,128)(2,1)} fusion(bf16[384,20,128]{0,2,1:T(8,128)(2,1)S(1)} %bitcast.59, f32[20,384,384]{1,2,0:T(8,128)} %fusion.49, f32[20,384,384]{1,2,0:T(8,128)} %get-tuple-element.26, f32[20,384]{1,0:T(8,128)S(1)} %get-tuple-element.25), kind=kOutput, calls=%fused_computation.35 | convolution fusion | flops 776609664 | bytes 27555840 | tf_op jit(solution)/shard_map/shqk,sqhd->skhd/dot_general | solution.py:96
  590.4 0.0 copy-start.3
  590.5 4.1 copy.46
  594.6 0.0 copy-done.3
  594.6 7.5 %fusion.29 = bf16[20,128,384]{2,1,0:T(8,128)(2,1)} fusion(bf16[384,20,128]{0,2,1:T(8,128)(2,1)S(1)} %bitcast.54, f32[20,384,384]{1,2,0:T(8,128)} %get-tuple-element.26, f32[20,384]{1,0:T(8,128)S(1)} %get-tuple-element.25), kind=kOutput, calls=%fused_computation.33 | convolution fusion | flops 761856000 | bytes 15759360 | tf_op jit(solution)/shard_map/shqk,sqhd->skhd/dot_general | solution.py:85
  602.1 4.0 copy.47
  606.1 0.0 all-to-all-done
  606.1 4.7 copy.56
  610.8 0.0 all-gather.5.cloned.1.call-done
  610.8 17.7 %fusion.50 = f32[320,2560]{1,0:T(8,128)} fusion(bf16[6144,320]{0,1:T(8,128)(2,1)} %bitcast.55, bf16[6144,2560]{0,1:T(8,128)(2,1)} %all-gather.5.cloned.1.call-done), kind=kOutput, calls=%fused_computation.51 | convolution fusion | flops 10066329600 | bytes 38666240 | tf_op jit(solution)/shard_map/dot_general | solution.py:78
  (3 shorter events, 0.0 us)
Async XLA Ops:
  7.2 2.9 copy-start.6
  7.2 236.9 %all-reduce.2.cloned.1.call-start = ((), (), s32[]{:S(2)}) async-start(), calls=%async_computation.1 | async-start | bytes 15728640 | tf_op jit(solution)/shard_map/psum | solution.py:56
  10.1 18.9 %copy-start.1 = (bf16[384,2560]{0,1:T(8,128)(2,1)}, bf16[384,2560]{0,1:T(8,128)(2,1)S(1)}, u32[]{:S(2)}) copy-start(bf16[384,2560]{0,1:T(8,128)(2,1)S(1)} %copy.35) | copy-start | bytes 5898244
  54.0 265.4 %all-gather.3.cloned.1.call-start = ((), (), s32[]{:S(2)}) async-start(), calls=%async_computation.2 | async-start | bytes 5898240 | tf_op jit(solution)/shard_map/all_gather | solution.py:72
  54.2 198.3 %copy-start.5 = (f32[2560]{0:T(1024)S(1)}, f32[2560]{0:T(1024)}, u32[]{:S(2)}) copy-start(f32[2560]{0:T(1024)} %param.15) | copy-start | bytes 30724
  247.5 17.9 %copy-start = (bf16[384,2560]{1,0:T(8,128)(2,1)}, bf16[384,2560]{1,0:T(8,128)(2,1)S(1)}, u32[]{:S(2)}) copy-start(bf16[384,2560]{1,0:T(8,128)(2,1)S(1)} %get-tuple-element.24) | copy-start | bytes 5898244
  265.5 345.3 %all-gather.5.cloned.1.call-start = ((), (), s32[]{:S(2)}) async-start(), calls=%async_computation.3 | async-start | bytes 33423360 | tf_op jit(solution)/shard_map/all_gather | solution.py:80
  325.7 280.4 %all-to-all-start = ((bf16[384,16,320]{0,2,1:T(8,128)(2,1)}), bf16[384,16,320]{0,2,1:T(8,128)(2,1)}, u32[]{:S(2)}, u32[]{:S(2)}) async-start(bf16[384,16,320]{0,2,1:T(8,128)(2,1)} %bitcast.50), calls=%async_computation | async-start | bytes 7864320 | tf_op jit(solution)/shard_map/all_to_all | solution.py:77
  534.5 4.2 copy-start.2
  566.6 4.1 copy-start.4
  590.4 4.1 copy-start.3
Sparse Core Ops, SparseCore 0:
  54.1 189.9 all-reduce.1
  265.6 53.7 all-gather.2
  321.5 231.1 all-gather.4
where the time goes:
time: 636 us; the launch traced here: 635 us
  waiting for transfers between devices  244 us (38%)
  blocking collectives  196 us (31%)
  matrix products  126 us (20%)
  local copies, waits for them, and re-layouts  38.5 us (6%)
  between operations  13.8 us (2%)
  other arithmetic  11.7 us (2%)
    psum x1, waiting for transfers between devices, shards(): full_sum = lax.psum(projected, 'tensor')  190 us
    psum x1, blocking collectives, shards(): grad_gain = lax.psum(jnp.sum(upstream_float * normed, axis=0), 'dp')  186 us
    all_gather x1, waiting for transfers between devices, shards(): grad_full = lax.all_gather(grad_residual, 'tensor', axis=1, tiled=True)  53.2 us
    unnamed x20, local copies, waits for them, and re-layouts  23.4 us
    dot_general x1, matrix products, shards(): jnp.einsum('shqk,skhd->sqhd', grad_scores, key_heads, preferred_element_t...  20.3 us
    dot_general x1, matrix products, shards(): jnp.einsum('shqk,sqhd->skhd', grad_scores, query_heads, preferred_element...  19.7 us
    dot_general x1, matrix products, shards(): jnp.dot(attended, out_weight.T, preferred_element_type=jnp.float32)  17.8 us
    dot_general x1, matrix products, shards(): lax.dot_general(received, lax.all_gather(attended, 'dp', axis=0, tiled=Tr...  17.7 us
  transfers between devices with their start and end apart: 4, of which 2 were waited for; matrix products, arithmetic and copies ran while one was open for 16% of the time, Pallas kernels for 0%

commit v1 on v0

v1 whole, which is shorter than its diff:
```python
import functools

import jax
import jax.numpy as jnp
from jax import lax
from jax.experimental import pallas as pl
from jax.experimental.pallas import tpu as pltpu
from jax.sharding import PartitionSpec as P

HEAD_DIM = 128
LEN = 384

epsilon = 1e-05
SCALE = HEAD_DIM ** (-0.5)
NT = (((1,), (1,)), ((), ()))
TN = (((0,), (0,)), ((), ()))


def dot(a, b, dims):
    return lax.dot_general(a, b, dims, preferred_element_type=jnp.float32)


def forward_kernel(heads, observed_ref, query_ref, key_ref, value_ref, probs_ref, attended_ref):
    observed = observed_ref[pl.program_id(0)]
    row = lax.broadcasted_iota(jnp.int32, (LEN, LEN), 0)
    column = lax.broadcasted_iota(jnp.int32, (LEN, LEN), 1)
    allowed = column <= jnp.maximum(row, observed - 1)
    for head in range(heads):
        span = slice(head * HEAD_DIM, (head + 1) * HEAD_DIM)
        scores = dot(query_ref[:, span], key_ref[:, span], NT) * SCALE
        masked = jnp.where(allowed, scores, -jnp.inf)
        weights = jnp.exp(masked - jnp.max(masked, axis=1, keepdims=True))
        probs = weights * (1.0 / jnp.sum(weights, axis=1, keepdims=True))
        low = probs.astype(jnp.bfloat16)
        probs_ref[head] = low
        attended_ref[:, span] = jnp.dot(
            low, value_ref[:, span], preferred_element_type=jnp.float32
        ).astype(jnp.bfloat16)


def backward_kernel(
    heads, probs_ref, query_ref, key_ref, value_ref, cotangent_ref, query_out, key_out, value_out
):
    for head in range(heads):
        span = slice(head * HEAD_DIM, (head + 1) * HEAD_DIM)
        low = probs_ref[head]
        cotangent = cotangent_ref[:, span]
        value_out[:, span] = dot(low, cotangent, TN).astype(jnp.bfloat16)
        grad_probs = dot(cotangent, value_ref[:, span], NT)
        probs = low.astype(jnp.float32)
        delta = jnp.sum(probs * grad_probs, axis=1, keepdims=True)
        grad_scores = (probs * (grad_probs - delta) * SCALE).astype(jnp.bfloat16)
        query_out[:, span] = jnp.dot(
            grad_scores, key_ref[:, span], preferred_element_type=jnp.float32
        ).astype(jnp.bfloat16)
        key_out[:, span] = dot(grad_scores, query_ref[:, span], TN).astype(jnp.bfloat16)


def head_group(head_count):
    return max(size for size in range(1, 6) if head_count % size == 0)


def specs(heads):
    rows = pl.BlockSpec((LEN, heads * HEAD_DIM), lambda s, h: (s, h))
    square = pl.BlockSpec((None, heads, LEN, LEN), lambda s, h: (s, h, 0, 0))
    return rows, square


def attend(observed, query_rows, key_rows, value_rows):
    tok_rows, width = query_rows.shape
    head_count, seq_count = width // HEAD_DIM, tok_rows // LEN
    heads = head_group(head_count)
    rows, square = specs(heads)
    pairs = seq_count * head_count * LEN * LEN
    return pl.pallas_call(
        functools.partial(forward_kernel, heads),
        grid=(seq_count, head_count // heads),
        in_specs=[pl.BlockSpec(memory_space=pltpu.SMEM), rows, rows, rows],
        out_specs=[square, rows],
        out_shape=[
            jax.ShapeDtypeStruct((seq_count, head_count, LEN, LEN), jnp.bfloat16),
            jax.ShapeDtypeStruct((tok_rows, width), jnp.bfloat16),
        ],
        cost_estimate=pl.CostEstimate(
            flops=4 * pairs * HEAD_DIM,
            bytes_accessed=2 * pairs + 8 * tok_rows * width,
            transcendentals=pairs,
        ),
        name="attend",
    )(observed, query_rows, key_rows, value_rows)


def attend_backward(probs, query_rows, key_rows, value_rows, cotangent):
    tok_rows, width = query_rows.shape
    head_count, seq_count = width // HEAD_DIM, tok_rows // LEN
    heads = head_group(head_count)
    rows, square = specs(heads)
    pairs = seq_count * head_count * LEN * LEN
    return pl.pallas_call(
        functools.partial(backward_kernel, heads),
        grid=(seq_count, head_count // heads),
        in_specs=[square, rows, rows, rows, rows],
        out_specs=[rows, rows, rows],
        out_shape=[jax.ShapeDtypeStruct((tok_rows, width), jnp.bfloat16)] * 3,
        cost_estimate=pl.CostEstimate(
            flops=8 * pairs * HEAD_DIM,
            bytes_accessed=2 * pairs + 14 * tok_rows * width,
            transcendentals=0,
        ),
        name="attend_backward",
    )(probs, query_rows, key_rows, value_rows, cotangent)


def sum_groups(groups, value):
    if groups & (groups - 1):
        return lax.psum(value, "dp")
    bit = 1
    while bit < groups:
        value = value + lax.ppermute(value, "dp", [(i, i ^ bit) for i in range(groups)])
        bit *= 2
    return value


def shards(
    groups,
    tensor_size,
    query_rows,
    key_rows,
    value_rows,
    action_mask,
    residual,
    out_weight,
    norm_gain,
    upstream,
    residual_grad,
):
    model_width = out_weight.shape[0]
    own_width = residual.shape[1]
    pair = tensor_size == 2
    swap = [(0, 1), (1, 0)]
    mine = lax.axis_index("tensor")

    def weight_rows(index):
        return lax.dynamic_slice_in_dim(out_weight, index * own_width, own_width, 0)

    def sum_pair(value):
        if pair:
            return value + lax.ppermute(value, "tensor", swap)
        return lax.psum(value, "tensor")

    observed = jnp.sum((action_mask == 0).astype(jnp.int32), axis=1)
    probs, attended = attend(observed, query_rows, key_rows, value_rows)
    attended_all = lax.all_gather(attended, "dp", axis=0, tiled=True)
    if pair:
        theirs = dot(attended, weight_rows(1 - mine), NT).astype(jnp.bfloat16)
        arriving = lax.ppermute(theirs, "tensor", swap)
        own = dot(attended, weight_rows(mine), NT)
        own_sum = own + arriving.astype(jnp.float32)
    else:
        own_sum = lax.psum_scatter(
            dot(attended, out_weight, NT), "tensor", scatter_dimension=1, tiled=True
        )
    layer_out = (own_sum + residual.astype(jnp.float32)).astype(jnp.bfloat16)
    out_float = layer_out.astype(jnp.float32)
    upstream_float = upstream.astype(jnp.float32)
    scaled = upstream_float * norm_gain[None, :]
    sums = sum_pair(
        jnp.stack([jnp.sum(out_float * out_float, axis=1), jnp.sum(scaled * out_float, axis=1)])
    )
    row_rms = jnp.sqrt(sums[0] / model_width + epsilon)[:, None]
    normed = out_float / row_rms
    row_inner = sums[1][:, None] / (row_rms * model_width)
    grad_residual = (
        residual_grad.astype(jnp.float32) + (scaled - normed * row_inner) / row_rms
    ).astype(jnp.bfloat16)
    if pair:
        other = lax.ppermute(grad_residual, "tensor", swap)
        first = mine == 0
        low_half = jnp.where(first, grad_residual, other)
        high_half = jnp.where(first, other, grad_residual)
        grad_full = jnp.concatenate([low_half, high_half], axis=1)
        grad_attended = jnp.dot(
            grad_residual, weight_rows(mine), preferred_element_type=jnp.float32
        ) + jnp.dot(other, weight_rows(1 - mine), preferred_element_type=jnp.float32)
    else:
        grad_full = lax.all_gather(grad_residual, "tensor", axis=1, tiled=True)
        grad_attended = jnp.dot(grad_full, out_weight, preferred_element_type=jnp.float32)
    grad_attended = grad_attended.astype(jnp.bfloat16)
    received = lax.all_to_all(grad_full, "dp", split_axis=1, concat_axis=0, tiled=True)
    gain_part = jnp.sum(upstream_float * normed, axis=0)
    grad_query, grad_key, grad_value = attend_backward(
        probs, query_rows, key_rows, value_rows, grad_attended
    )
    grad_query, gain_part = lax.optimization_barrier((grad_query, gain_part))
    grad_gain = sum_groups(groups, gain_part)
    grad_out_weight = dot(received, attended_all, TN)
    return layer_out, grad_residual, grad_query, grad_key, grad_value, grad_out_weight, grad_gain


def solution(mesh):
    rows = P("dp", "tensor")
    return jax.shard_map(
        functools.partial(shards, mesh.shape["dp"], mesh.shape["tensor"]),
        mesh=mesh,
        in_specs=(
            rows,
            rows,
            rows,
            P("dp", None),
            rows,
            P(None, "tensor"),
            P("tensor"),
            rows,
            rows,
        ),
        out_specs=(rows, rows, rows, rows, rows, rows, P("tensor")),
        check_vma=False,
    )
```

time: 636 us -> 297 us (0.47)
  blocking collectives: 196 us -> 0 us
  waiting for transfers between devices: 244 us -> 143 us
  matrix products: 126 us -> 72.2 us
  local copies, waits for them, and re-layouts: 38.5 us -> 11 us
  Pallas kernels: 0 us -> 26.9 us
  starting transfers between devices: 5.96 us -> 21.2 us
    psum x3 -> x0, blocking collectives: 196 us -> none  [the longest x1 186 us: shards(): grad_gain = lax.psum(jnp.sum(upstream_float * normed, axis=0), 'dp')]
    psum x1 -> x0, waiting for transfers between devices: 190 us -> none  [shards(): full_sum = lax.psum(projected, 'tensor')]
    ppermute x0 -> x7, waiting for transfers between devices: none -> 143 us  [the longest x4 56.3 us: sum_groups(): lax.ppermute(value, 'dp', [(i, i ^ bit) for i in range(groups)])]
    all_gather x2 -> x1, waiting for transfers between devices: 53.2 us -> 0.01 us  [shards(): attended_all = lax.all_gather(attended, 'dp', axis=0, tiled=True)]
    dot_general x8 -> x5, matrix products: 115 us -> 72.2 us  [the longest x3 52.4 us: dot(): return lax.dot_general(a, b, dims, preferred_element_type=jnp.float32)]
    pallas_call x0 -> x2, Pallas kernels: none -> 26.9 us  [the longest x1 13.9 us: attend_backward(): pl.pallas_call(functools.partial(backward_kernel, heads), grid=(seq_count...]
    unnamed x20 -> x12, local copies, waits for them, and re-layouts: 23.4 us -> 0.03 us
    ppermute x0 -> x7, starting transfers between devices: none -> 15.2 us  [the longest x4 8.6 us: sum_groups(): lax.ppermute(value, 'dp', [(i, i ^ bit) for i in range(groups)])]
  transfers between devices with their start and end apart: 4 -> 9, of which waited for: 2 -> 7; matrix products, arithmetic and copies ran while one was open for 16% -> 24% of each run, Pallas kernels for 0% -> 5%
where the time goes in v1:
time: 297 us; the launch traced here: 296 us
  waiting for transfers between devices  143 us (48%)
  matrix products  72.2 us (24%)
  Pallas kernels  26.9 us (9%)
  starting transfers between devices  21.2 us (7%)
  between operations  14.2 us (5%)
  local copies, waits for them, and re-layouts  11 us (4%)
  other arithmetic  8.16 us (3%)
    ppermute x4, waiting for transfers between devices, sum_groups(): lax.ppermute(value, 'dp', [(i, i ^ bit) for i in range(groups)])  56.3 us
    dot_general x3, matrix products, dot(): return lax.dot_general(a, b, dims, preferred_element_type=jnp.float32)  52.4 us
    ppermute x1, waiting for transfers between devices, shards(): arriving = lax.ppermute(theirs, 'tensor', swap)  43.1 us
    ppermute x1, waiting for transfers between devices, shards(): other = lax.ppermute(grad_residual, 'tensor', swap)  41.6 us
    pallas_call x1, Pallas kernels, attend_backward(): pl.pallas_call(functools.partial(backward_kernel, heads), grid=(seq_count...  13.9 us
    pallas_call x1, Pallas kernels, attend(): pl.pallas_call(functools.partial(forward_kernel, heads), grid=(seq_count,...  13 us
    dot_general x1, matrix products, shards(): jnp.dot(other, weight_rows(1 - mine), preferred_element_type=jnp.float32)  11.5 us
    ppermute x4, starting transfers between devices, sum_groups(): lax.ppermute(value, 'dp', [(i, i ^ bit) for i in range(groups)])  8.6 us
  transfers between devices with their start and end apart: 9, of which 7 were waited for; matrix products, arithmetic and copies ran while one was open for 24% of the time, Pallas kernels for 5%

profile of v1, /device:TPU:0, one launch (start us, length us, event | category | flops | bytes accessed | tf_op | source)
XLA Modules:
  0.0 296.5 jit_solution(4896069805837783981)
XLA Ops:
  7.2 0.0 all-gather.2.cloned.1.call-start
  7.2 1.3 fusion.24
  8.5 13.0 %attend.1 = (bf16[1,20,384,384]{3,2,1,0:T(8,128)(2,1)}, bf16[384,2560]{1,0:T(8,128)(2,1)}) custom-call(s32[1]{0:T(128)} %bitcast.observed_ref, bf16[384,2560]{1,0:T(8,128)(2,1)} %query_ref.3, bf16[384,2560]{1,0:T(8,128)(2,1)} %key_ref.3, bf16[384,2560]{1,0:T(8,128)(2,1)} %value_ref.3), custom_call_target="tpu_custom_call" | custom-call | flops 1509949440 | bytes 13762560 | tf_op jit(solution)/shard_map/attend/pallas_call | solution.py:75
  21.5 0.0 all-gather.2.cloned.1.call-update
  21.6 0.0 copy-start.1
  21.6 0.0 copy-start.5
  21.6 14.9 %fusion.15 = bf16[384,2560]{1,0:T(8,128)(2,1)} fusion(bf16[384,2560]{1,0:T(8,128)(2,1)} %get-tuple-element.14, bf16[5120,2560]{1,0:T(8,128)(2,1)} %param.14, s32[]{:T(128)S(6)} %select_n.21), kind=kOutput, calls=%fused_computation.16 | convolution fusion | flops 5034147840 | bytes 17039364 | tf_op jit(solution)/shard_map/dot_general | solution.py:20
  36.5 3.0 %collective-permute-start = (bf16[384,2560]{1,0:T(8,128)(2,1)}, bf16[384,2560]{1,0:T(8,128)(2,1)}, u32[]{:S(2)}, u32[]{:S(2)}) collective-permute-start(bf16[384,2560]{1,0:T(8,128)(2,1)} %fusion.15), channel_id=1, source_target_pairs={{0,1},{1,0},{2,3},{3,2},{4,5},{5,4},{6,7},{7,6},{8,9},{9,8},{10,11... | collective-permute-start | bytes 5898248 | tf_op jit(solution)/shard_map/ppermute | solution.py:156
  39.5 0.0 copy-start.2
  39.5 0.0 copy-start.3
  39.5 43.1 %collective-permute-done = bf16[384,2560]{1,0:T(8,128)(2,1)} collective-permute-done((bf16[384,2560]{1,0:T(8,128)(2,1)}, bf16[384,2560]{1,0:T(8,128)(2,1)}, u32[]{:S(2)}, u32[]{:S(2)}) %collective-permute-start) | collective-permute-done | bytes 1966112 | tf_op jit(solution)/shard_map/ppermute | solution.py:156
  82.6 0.0 copy-done.1
  82.6 0.0 copy-done.5
  82.6 19.3 %fusion.21 = (f32[384]{0:T(512)S(1)}, f32[384]{0:T(512)S(1)}, bf16[384,2560]{1,0:T(8,128)(2,1)S(1)}) fusion(f32[2560]{0:T(1024)S(1)} %copy-done.5, bf16[384,2560]{1,0:T(8,128)(2,1)} %param.16, bf16[384,2560]{1,0:T(8,128)(2,1)} %param.13, bf16[384,2560]{1,0:T(8,128)(2,1)} %collective-permute-done, bf16[384,2560]{1,0:T(8,128)(2,1)S(1)} %copy-done.1, ...), kind=kOutput, calls=%fused_computation.20 | convolution fusion | flops 5044960256 | bytes 22950916 | tf_op jit(solution)/shard_map/dot_general | solution.py:20
  101.9 0.0 copy-start.4
  102.0 1.8 collective-permute-start.1
  103.8 1.9 collective-permute-done.1
  105.7 0.0 copy-done.2
  105.7 0.0 copy-done.3
  105.7 2.0 fusion.20
  107.7 0.0 copy-done.4
  107.7 0.0 copy-start
  107.7 1.8 collective-permute-start.2
  109.5 41.6 %collective-permute-done.2 = bf16[384,2560]{1,0:T(8,128)(2,1)} collective-permute-done((bf16[384,2560]{1,0:T(8,128)(2,1)S(1)}, bf16[384,2560]{1,0:T(8,128)(2,1)}, u32[]{:S(2)}, u32[]{:S(2)}) %collective-permute-start.2) | collective-permute-done | bytes 1966112 | tf_op jit(solution)/shard_map/ppermute | solution.py:177
  151.1 1.8 broadcast_select_fusion.1
  153.0 2.3 pad_maximum_fusion
  155.3 6.2 %copy.16 = bf16[384,5120]{0,1:T(8,128)(2,1)} copy(bf16[384,5120]{1,0:T(8,128)(2,1)} %pad_maximum_fusion) | data formatting | bytes 7864320 | tf_op jit(solution)/shard_map/concatenate | solution.py:181
  161.6 5.9 %all-to-all-start = ((bf16[384,16,320]{0,2,1:T(8,128)(2,1)}), bf16[384,16,320]{0,2,1:T(8,128)(2,1)}, u32[]{:S(2)}, u32[]{:S(2)}) async-start(bf16[384,16,320]{0,2,1:T(8,128)(2,1)} %bitcast.11), calls=%async_computation | async-start | bytes 7864320 | tf_op jit(solution)/shard_map/all_to_all | solution.py:189
  167.5 0.0 copy-done
  167.5 8.3 %fusion.4 = f32[384,2560]{1,0:T(8,128)S(1)} fusion(bf16[384,2560]{1,0:T(8,128)(2,1)S(1)} %get-tuple-element.26, bf16[5120,2560]{1,0:T(8,128)(2,1)} %param.14, s32[]{:T(128)S(6)} %select_n.20), kind=kOutput, calls=%fused_computation.4 | convolution fusion | flops 5033164800 | bytes 19005444 | tf_op jit(solution)/shard_map/dot_general | solution.py:182
  175.8 11.5 %fusion.12.cotangent_ref = bf16[384,2560]{1,0:T(8,128)(2,1)} fusion(f32[384,2560]{1,0:T(8,128)S(1)} %fusion.4, bf16[384,2560]{1,0:T(8,128)(2,1)} %collective-permute-done.2, bf16[5120,2560]{1,0:T(8,128)(2,1)} %param.14, s32[]{:T(128)S(6)} %select_n.21), kind=kOutput, calls=%fused_computation.15 | convolution fusion | flops 5035130880 | bytes 20971524 | tf_op jit(solution)/shard_map/dot_general | solution.py:184
  187.3 13.9 %attend_backward.1 = (bf16[384,2560]{1,0:T(8,128)(2,1)}, bf16[384,2560]{1,0:T(8,128)(2,1)}, bf16[384,2560]{1,0:T(8,128)(2,1)}) custom-call(bf16[1,20,384,384]{3,2,1,0:T(8,128)(2,1)} %get-tuple-element.15.probs_ref, bf16[384,2560]{1,0:T(8,128)(2,1)} %query_ref.3, bf16[384,2560]{1,0:T(8,128)(2,1)} %key_ref.3, bf16[384,2560]{1,0:T(8,128)(2,1)} %value_ref.3, ...), custom_call_target="tpu_custom_call" | custom-call | flops 3019898880 | bytes 19660800 | tf_op jit(solution)/shard_map/attend_backward/pallas_call | solution.py:99
  201.2 0.3 collective-permute-start.3
  201.6 0.8 collective-permute-done.3
  202.4 2.0 collective-permute-start.4
  204.4 1.7 collective-permute-done.4
  206.2 1.8 collective-permute-start.5
  208.0 33.9 %collective-permute-done.5 = f32[2560]{0:T(1024)S(1)} collective-permute-done((f32[2560]{0:T(1024)S(1)}, f32[2560]{0:T(1024)S(1)}, u32[]{:S(2)}, u32[]{:S(2)}) %collective-permute-start.5) | collective-permute-done | bytes 10272 | tf_op jit(solution)/shard_map/ppermute | solution.py:119
  241.9 4.4 %collective-permute-start.6 = (f32[2560]{0:T(1024)S(1)}, f32[2560]{0:T(1024)S(1)}, u32[]{:S(2)}, u32[]{:S(2)}) collective-permute-start(f32[2560]{0:T(1024)S(1)} %add.60), channel_id=1, source_target_pairs={{0,16},{2,18},{4,20},{6,22},{8,24},{10,26},{12,28},{14,30},{16,0},... | collective-permute-start | bytes 30728 | tf_op jit(solution)/shard_map/ppermute | solution.py:119
  246.3 19.8 %collective-permute-done.6 = f32[2560]{0:T(1024)S(1)} collective-permute-done((f32[2560]{0:T(1024)S(1)}, f32[2560]{0:T(1024)S(1)}, u32[]{:S(2)}, u32[]{:S(2)}) %collective-permute-start.6) | collective-permute-done | bytes 10272 | tf_op jit(solution)/shard_map/ppermute | solution.py:119
  266.1 0.6 add.61
  266.7 0.0 all-to-all-done
  266.7 4.7 %copy.18 = bf16[16,40,8,384]{3,2,0,1:T(8,128)(2,1)} copy(bf16[16,40,8,384]{3,2,1,0:T(8,128)(2,1)} %bitcast.3) | data formatting | bytes 7864320 | tf_op jit(solution)/shard_map/all_to_all | solution.py:189
  271.4 0.0 all-gather.2.cloned.1.call-done
  271.4 18.2 %fusion.35 = f32[320,2560]{1,0:T(8,128)} fusion(bf16[6144,320]{0,1:T(8,128)(2,1)} %bitcast.12, bf16[6144,2560]{1,0:T(8,128)(2,1)} %all-gather.2.cloned.1.call-done), kind=kOutput, calls=%fused_computation.41 | convolution fusion | flops 10066329600 | bytes 38666240 | tf_op jit(solution)/shard_map/dot_general | solution.py:20
  (9 shorter events, 0.1 us)
Async XLA Ops:
  7.2 264.2 %all-gather.2.cloned.1.call-start = ((), (), s32[]{:S(2)}) async-start(), calls=%async_computation.1 | async-start | bytes 33423360 | tf_op jit(solution)/shard_map/all_gather | solution.py:153
  21.6 61.0 %copy-start.1 = (bf16[384,2560]{1,0:T(8,128)(2,1)S(1)}, bf16[384,2560]{1,0:T(8,128)(2,1)}, u32[]{:S(2)}) copy-start(bf16[384,2560]{1,0:T(8,128)(2,1)} %get-tuple-element.14) | copy-start | bytes 5898244
  21.6 61.0 %copy-start.5 = (f32[2560]{0:T(1024)S(1)}, f32[2560]{0:T(1024)}, u32[]{:S(2)}) copy-start(f32[2560]{0:T(1024)} %param.15) | copy-start | bytes 30724
  36.5 46.1 %collective-permute-start = (bf16[384,2560]{1,0:T(8,128)(2,1)}, bf16[384,2560]{1,0:T(8,128)(2,1)}, u32[]{:S(2)}, u32[]{:S(2)}) collective-permute-start(bf16[384,2560]{1,0:T(8,128)(2,1)} %fusion.15), channel_id=1, source_target_pairs={{0,1},{1,0},{2,3},{3,2},{4,5},{5,4},{6,7},{7,6},{8,9},{9,8},{10,11... | collective-permute-start | bytes 5898248 | tf_op jit(solution)/shard_map/ppermute | solution.py:156
  39.5 66.2 %copy-start.2 = (bf16[384,2560]{1,0:T(8,128)(2,1)S(1)}, bf16[384,2560]{1,0:T(8,128)(2,1)}, u32[]{:S(2)}) copy-start(bf16[384,2560]{1,0:T(8,128)(2,1)} %param.16) | copy-start | bytes 5898244
  39.5 66.2 %copy-start.3 = (bf16[384,2560]{1,0:T(8,128)(2,1)S(1)}, bf16[384,2560]{1,0:T(8,128)(2,1)}, u32[]{:S(2)}) copy-start(bf16[384,2560]{1,0:T(8,128)(2,1)} %param.17) | copy-start | bytes 5898244
  101.9 5.8 %copy-start.4 = (bf16[384,2560]{1,0:T(8,128)(2,1)}, bf16[384,2560]{1,0:T(8,128)(2,1)S(1)}, u32[]{:S(2)}) copy-start(bf16[384,2560]{1,0:T(8,128)(2,1)S(1)} %get-tuple-element.29) | copy-start | bytes 5898244
  102.0 3.7 %collective-permute-start.1 = (f32[2,384]{1,0:T(2,128)S(1)}, f32[2,384]{1,0:T(2,128)S(1)}, u32[]{:S(2)}, u32[]{:S(2)}) collective-permute-start(f32[2,384]{1,0:T(2,128)S(1)} %pad_maximum_fusion.1), channel_id=1, source_target_pairs={{0,1},{1,0},{2,3},{3,2},{4,5},{5,4},{6,7},{7,6},{8,9},{9,8},{10,11... | collective-permute-start | bytes 9224 | tf_op jit(solution)/shard_map/ppermute | solution.py:148
  107.7 59.8 %copy-start = (bf16[384,2560]{1,0:T(8,128)(2,1)}, bf16[384,2560]{1,0:T(8,128)(2,1)S(1)}, u32[]{:S(2)}) copy-start(bf16[384,2560]{1,0:T(8,128)(2,1)S(1)} %get-tuple-element.26) | copy-start | bytes 5898244
  107.7 43.4 %collective-permute-start.2 = (bf16[384,2560]{1,0:T(8,128)(2,1)S(1)}, bf16[384,2560]{1,0:T(8,128)(2,1)}, u32[]{:S(2)}, u32[]{:S(2)}) collective-permute-start(bf16[384,2560]{1,0:T(8,128)(2,1)S(1)} %get-tuple-element.26), channel_id=1, source_target_pairs={{0,1},{1,0},{2,3},{3,2},{4,5},{5,4},{6,7},{7,6},{8,9},{9,8},{10,11... | collective-permute-start | bytes 5898248 | tf_op jit(solution)/shard_map/ppermute | solution.py:177
  161.6 105.2 %all-to-all-start = ((bf16[384,16,320]{0,2,1:T(8,128)(2,1)}), bf16[384,16,320]{0,2,1:T(8,128)(2,1)}, u32[]{:S(2)}, u32[]{:S(2)}) async-start(bf16[384,16,320]{0,2,1:T(8,128)(2,1)} %bitcast.11), calls=%async_computation | async-start | bytes 7864320 | tf_op jit(solution)/shard_map/all_to_all | solution.py:189
  201.2 1.2 collective-permute-start.3
  202.4 3.7 %collective-permute-start.4 = (f32[2560]{0:T(1024)S(1)}, f32[2560]{0:T(1024)S(1)}, u32[]{:S(2)}, u32[]{:S(2)}) collective-permute-start(f32[2560]{0:T(1024)S(1)} %add.58), channel_id=1, source_target_pairs={{0,4},{2,6},{4,0},{6,2},{8,12},{10,14},{12,8},{14,10},{16,20},{18,... | collective-permute-start | bytes 30728 | tf_op jit(solution)/shard_map/ppermute | solution.py:119
  206.2 35.8 %collective-permute-start.5 = (f32[2560]{0:T(1024)S(1)}, f32[2560]{0:T(1024)S(1)}, u32[]{:S(2)}, u32[]{:S(2)}) collective-permute-start(f32[2560]{0:T(1024)S(1)} %add.59), channel_id=1, source_target_pairs={{0,8},{2,10},{4,12},{6,14},{8,0},{10,2},{12,4},{14,6},{16,24},{18,... | collective-permute-start | bytes 30728 | tf_op jit(solution)/shard_map/ppermute | solution.py:119
  241.9 24.2 %collective-permute-start.6 = (f32[2560]{0:T(1024)S(1)}, f32[2560]{0:T(1024)S(1)}, u32[]{:S(2)}, u32[]{:S(2)}) collective-permute-start(f32[2560]{0:T(1024)S(1)} %add.60), channel_id=1, source_target_pairs={{0,16},{2,18},{4,20},{6,22},{8,24},{10,26},{12,28},{14,30},{16,0},... | collective-permute-start | bytes 30728 | tf_op jit(solution)/shard_map/ppermute | solution.py:119
Sparse Core Ops, SparseCore 0:
  21.7 189.3 all-gather.1
